TPU v7x, 256 devices: a whole 4x4x8 slice. The times are simulated.
256 devices in a mesh: slab: 128 (over x, z, y), pencil: 2 (over core).
Axes of the slice: x: 4, y: 4, z: 8, core: 2. Of those that a mesh axis runs over, the one named last changes fastest.
Arguments:
- density: float32 [768, 768, 384], P('slab', 'pencil'), may hold values from 0 to 1
- cell_kind: int32 [768, 768, 384], P('slab', 'pencil'), may hold values from 0 to 2
- sharpness: float32 [1], replicated, may hold values from 48 to 96
- fraction: float32 [1], replicated, may hold values from 0.36 to 0.41
Outputs:
- physical: float32 [768, 768, 384], P('slab', 'pencil')
- threshold: float32 [1], replicated
Inputs may be any that keep to these rules, and one draw needn't show every extreme that they name: `cell_kind`: each cell is a design, void or solid cell.
All inputs are finite; a program needn't handle non-finite values.
Results may differ from a plain program's by a relative error of at most 0.0003.
Values sent between devices are 32-bit elements; how exact they have to be, the bound alone decides.
A program may use at most 128 MiB of HBM per device.

v0:
```python
import functools

import jax
import jax.numpy as jnp
from jax import lax
from jax.experimental import pallas as pl
from jax.experimental.pallas import tpu as pltpu
from jax.sharding import PartitionSpec as P

RADIUS = 5
ITERS = 3
CHUNK = 16
PAD = 8
WINDOW = 4
LEAD = 8
LANES = 128
FAR = 1.0e6
MESH = pl.DeviceIdType.MESH


def box(values):
    pairs = [a + b for a, b in zip(values[:-1], values[1:])]
    return [pairs[k] + pairs[k + 2] + pairs[k + 4] for k in range(len(values) - RADIUS)]


def triangle(k):
    k = jnp.maximum(k, 0)
    return (k * (k + 1)) // 2


def coverage(index, whole):
    full = (RADIUS + 1) * (RADIUS + 1)
    return (full - triangle(RADIUS - index) - triangle(RADIUS + 1 + index - whole)).astype(jnp.float32)


def split(x):
    high = x.astype(jnp.bfloat16)
    return high, (x - high.astype(jnp.float32)).astype(jnp.bfloat16)


def band(shape, shift):
    row = lax.broadcasted_iota(jnp.int32, shape, 0)
    col = lax.broadcasted_iota(jnp.int32, shape, 1)
    return jnp.maximum(RADIUS + 1 - jnp.abs(col - shift - row), 0).astype(jnp.float32).astype(jnp.bfloat16)


def folded(x):
    tiles = [
        x[i : i + 8, j : j + LANES] for i in range(0, x.shape[0], 8) for j in range(0, x.shape[1], LANES)
    ]
    while len(tiles) > 1:
        tiles = [sum(tiles[i : i + 2][1:], tiles[i]) for i in range(0, len(tiles), 2)]
    return tiles[0]


def kernel(slabs, pencils, beta_ref, fraction_ref, density, kind, coded, level_out, own, near, far, kinds,
           along_z, x_band, acc, parts, x_send, x_recv, b_send, b_recv, f_send, f_recv, h_send, h_recv, local_sem,
           r_send, r_recv):
    depth, rows, cols = density.shape
    steps = rows // CHUNK
    lead = min(LEAD, steps)
    lag = lead + 1
    slab = lax.axis_index("slab")
    pencil = lax.axis_index("pencil")
    even = slab % 2 == 0
    first = pencil == 0
    devices = slabs * pencils
    me = slab * pencils + pencil

    barrier = pltpu.get_barrier_semaphore()

    def greet(k, carry):
        there = slab + (slabs - k)
        there = there - jnp.where(there >= slabs, slabs, 0)
        for core in range(pencils):
            pl.semaphore_signal(barrier, inc=1, device_id=(there, core), device_id_type=MESH)
        return carry

    lax.fori_loop(1, slabs, greet, 0, unroll=15 if slabs % 15 == 1 else 1)
    pl.semaphore_signal(barrier, inc=1, device_id=(slab, 1 - pencil), device_id_type=MESH)

    partner = slab + jnp.where(even, 1, -1)
    target = slab + jnp.where(even, 2, -2)
    source = slab - jnp.where(even, 2, -2)
    has_target = (target >= 0) & (target < slabs)
    has_source = (source >= 0) & (source < slabs)
    target = jnp.clip(target, 0, slabs - 1)
    sibling = 1 - pencil
    halo = pl.multiple_of(jnp.where(first, PAD + rows, 0), 8)
    edge = pl.multiple_of(jnp.where(first, 0, PAD + rows), 8)
    there = pl.multiple_of(jnp.where(first, 0, PAD + rows), 8)
    mine = pl.multiple_of(jnp.where(first, rows, PAD), 8)

    def row_of(k):
        return pl.multiple_of(jnp.where(first, steps - 1 - k, k) * CHUNK, CHUNK)

    def x_copy(k):
        r = row_of(k)
        layers = pl.ds(jnp.where(even, 0, depth - RADIUS), RADIUS)
        return pltpu.make_async_remote_copy(
            density.at[layers, pl.ds(r, CHUNK), :], near.at[layers, pl.ds(r + PAD, CHUNK), :],
            x_send.at[k], x_recv.at[k], device_id=(partner, pencil), device_id_type=MESH)

    def b_copy(k):
        r = row_of(k)
        layers = pl.ds(jnp.where(even, RADIUS, 0), depth - RADIUS)
        return pltpu.make_async_remote_copy(
            density.at[layers, pl.ds(r, CHUNK), :], near.at[layers, pl.ds(r + PAD, CHUNK), :],
            b_send.at[k], b_recv.at[k], device_id=(partner, pencil), device_id_type=MESH)

    def f_copy(k):
        r = row_of(k)
        start = jnp.where(even, depth - RADIUS, 0)
        return pltpu.make_async_remote_copy(
            near.at[pl.ds(start, RADIUS), pl.ds(r + PAD, CHUNK), :], far.at[:, pl.ds(r + PAD, CHUNK), :],
            f_send.at[k], f_recv.at[k], device_id=(target, pencil), device_id_type=MESH)

    def halo_copy(index, src, dst):
        return pltpu.make_async_remote_copy(
            src, dst, h_send.at[index], h_recv.at[index], device_id=(slab, sibling), device_id_type=MESH)

    own_row = pl.multiple_of(jnp.where(first, rows - PAD, 0), 8)
    own_halo = halo_copy(0, density.at[:, pl.ds(own_row, PAD), :], own.at[:, pl.ds(there, PAD), :])
    near_halo = halo_copy(1, near.at[:, pl.ds(mine, PAD), :], near.at[:, pl.ds(there, PAD), :])
    far_halo = halo_copy(2, far.at[:, pl.ds(mine, PAD), :], far.at[:, pl.ds(there, PAD), :])
    own_load = pltpu.make_async_copy(density, own.at[:, pl.ds(PAD, rows), :], local_sem.at[0])
    kind_load = pltpu.make_async_copy(kind, kinds, local_sem.at[1])

    own_load.start()
    kind_load.start()
    pl.semaphore_wait(barrier, devices - 1)
    for k in range(min(WINDOW, steps)):
        x_copy(k).start()
    own_halo.start()

    x_band[...] = band((cols, cols), 0)
    acc[...] = jnp.zeros_like(acc)
    along_z[:, pl.ds(edge, PAD), :] = jnp.zeros((depth, PAD, cols), jnp.float32)

    @pl.when(jnp.logical_not(has_source))
    def _():
        @pl.loop(0, RADIUS)
        def _(k):
            far[k] = jnp.zeros(far.shape[1:], jnp.float32)

    beta = beta_ref[0]

    def filter_z(start, count):
        for r in range(0, count, 8):
            for c in range(0, cols, LANES):
                at = (pl.ds(pl.multiple_of(start + r, 8), 8), pl.ds(c, LANES))
                values = [far[jnp.where(even, m, RADIUS - 1 - m), at[0], at[1]] for m in range(RADIUS)]
                values += [own[jnp.where(even, i, depth - 1 - i), at[0], at[1]] for i in range(depth)]
                values += [near[jnp.where(even, i, depth - 1 - i), at[0], at[1]] for i in range(RADIUS)]
                for i, out in enumerate(box(box(values))):
                    along_z[jnp.where(even, i, depth - 1 - i), at[0], at[1]] = out

    def filter_yx(j):
        r = row_of(j)
        y_band = band((CHUNK, CHUNK + 2 * PAD), PAD)
        pieces = []
        for layer in range(depth):
            high, low = split(along_z[layer, pl.ds(r, CHUNK + 2 * PAD), :])
            pieces.append(jnp.dot(y_band, high, preferred_element_type=jnp.float32)
                          + jnp.dot(y_band, low, preferred_element_type=jnp.float32))
        high, low = split(jnp.concatenate(pieces, axis=0))
        smoothed = (jnp.dot(high, x_band[...], preferred_element_type=jnp.float32)
                    + jnp.dot(low, x_band[...], preferred_element_type=jnp.float32))
        row = lax.broadcasted_iota(jnp.int32, (CHUNK, cols), 0) + (pencil * rows + r)
        col = lax.broadcasted_iota(jnp.int32, (CHUNK, cols), 1)
        cover_y = coverage(row, rows * pencils)
        cover_x = coverage(col, cols)
        for layer in range(depth):
            depth_index = jnp.full((1, cols), slab * depth + layer, jnp.int32)
            cover = coverage(depth_index, slabs * depth) * cover_y * cover_x
            filtered = smoothed[layer * CHUNK : (layer + 1) * CHUNK] / cover
            which = kinds[layer, pl.ds(r, CHUNK), :]
            value = jnp.where(which == 0, filtered, jnp.where(which == 2, FAR, -FAR))
            coded[layer, pl.ds(r, CHUNK), :] = value
            tangent = jnp.tanh(beta * (value - 0.5))
            acc[0] += folded(tangent)
            acc[1] += folded(1.0 - tangent * tangent)

    @pl.loop(0, steps + lag + 1)
    def _(k):
        @pl.when(k < steps)
        def _():
            x_copy(k).wait_recv()

            @pl.when(has_target)
            def _():
                f_copy(k).start()

        @pl.when(k + WINDOW < steps)
        def _():
            x_copy(k + WINDOW).start()

            @pl.when(k + WINDOW >= lead)
            def _():
                b_copy(k + WINDOW - lead).start()

        @pl.when(k + WINDOW == steps)
        def _():
            @pl.loop(max(steps - lead, 0), steps)
            def _(j):
                b_copy(j).start()

        @pl.when((k >= lag) & (k < steps + lag))
        def _():
            b_copy(k - lag).wait_recv()

            @pl.when(k == lag)
            def _():
                near_halo.start()

            @pl.when(has_source)
            def _():
                f_copy(k - lag).wait_recv()

                @pl.when(k == lag)
                def _():
                    far_halo.start()

            @pl.when(k == lag)
            def _():
                own_load.wait()
                kind_load.wait()

            filter_z(row_of(k - lag) + PAD, CHUNK)

        @pl.when(k == lag + 1)
        def _():
            own_halo.wait_recv()
            near_halo.wait_recv()

            @pl.when(has_source)
            def _():
                far_halo.wait_recv()

            filter_z(halo, PAD)

        @pl.when(k >= lag + 1)
        def _():
            filter_yx(k - lag - 1)

    cells = float(devices) * float(depth * rows * cols)
    level = jnp.full((1, 1), 0.5, jnp.float32)
    for step in range(ITERS):
        if step:
            center = jnp.broadcast_to(level, (8, cols))

            def body(i, carry):
                total, bend = carry
                for layer in range(depth):
                    tangent = jnp.tanh(beta * (coded[layer, pl.ds(pl.multiple_of(i * 8, 8), 8), :] - center))
                    total = total + tangent
                    bend = bend + (1.0 - tangent * tangent)
                return total, bend

            zero = jnp.zeros((8, cols), jnp.float32)
            total, bend = lax.fori_loop(0, rows // 8, body, (zero, zero), unroll=2)
            total, bend = folded(total), folded(bend)
        else:
            total, bend = acc[0], acc[1]
        parts[step, me] = jnp.concatenate(
            [jnp.sum(total, axis=0, keepdims=True), jnp.sum(bend, axis=0, keepdims=True)], axis=0)

        def send(there, core):
            pltpu.make_async_remote_copy(
                parts.at[step, me], parts.at[step, me], r_send.at[step], r_recv.at[step],
                device_id=(there, core), device_id_type=MESH).start()

        def send_all(k, carry):
            there = slab + (slabs - k)
            there = there - jnp.where(there >= slabs, slabs, 0)
            for core in range(pencils):
                send(there, core)
            return carry

        lax.fori_loop(1, slabs, send_all, 0, unroll=15 if slabs % 15 == 1 else 1)
        send(slab, sibling)

        most = parts.at[step, pl.ds(0, devices - 1)]
        pltpu.make_async_copy(most, most, r_recv.at[step]).wait()
        both = jnp.sum(jnp.sum(parts[step], axis=0), axis=1, keepdims=True)
        volume = 0.5 * (cells + both[0:1])
        slope = cells + 0.5 * beta * both[1:2]
        level = level + (volume - fraction_ref[0] * cells) / slope
    level_out[...] = jnp.broadcast_to(level, level_out.shape)

    @pl.loop(0, steps)
    def _(k):
        x_copy(k).wait_send()
        b_copy(k).wait_send()

        @pl.when(has_target)
        def _():
            f_copy(k).wait_send()

    own_halo.wait_send()
    near_halo.wait_send()

    @pl.when(has_source)
    def _():
        far_halo.wait_send()

    for step in range(ITERS):
        most = parts.at[step, pl.ds(0, devices - 1)]
        pltpu.make_async_copy(most, most, r_send.at[step]).wait()


def solution(mesh):
    slabs, pencils = mesh.shape["slab"], mesh.shape["pencil"]

    def local(density, cell_kind, sharpness, fraction):
        depth, rows, cols = density.shape
        steps = rows // CHUNK
        wide = rows + 2 * PAD
        coded, level = pl.pallas_call(
            functools.partial(kernel, slabs, pencils),
            out_shape=(jax.ShapeDtypeStruct(density.shape, jnp.float32), jax.ShapeDtypeStruct((1, LANES), jnp.float32)),
            in_specs=[pl.BlockSpec(memory_space=pltpu.SMEM)] * 2 + [pl.BlockSpec(memory_space=pltpu.HBM)] * 2,
            out_specs=(pl.BlockSpec(memory_space=pltpu.VMEM), pl.BlockSpec(memory_space=pltpu.VMEM)),
            scratch_shapes=[
                pltpu.VMEM((depth, wide, cols), jnp.float32),
                pltpu.VMEM((depth, wide, cols), jnp.float32),
                pltpu.VMEM((RADIUS, wide, cols), jnp.float32),
                pltpu.VMEM((depth, rows, cols), jnp.int32),
                pltpu.VMEM((depth, wide, cols), jnp.float32),
                pltpu.VMEM((cols, cols), jnp.bfloat16),
                pltpu.VMEM((2, 8, LANES), jnp.float32),
                pltpu.VMEM((ITERS, slabs * pencils, 2, LANES), jnp.float32),
                pltpu.SemaphoreType.DMA((steps,)),
                pltpu.SemaphoreType.DMA((steps,)),
                pltpu.SemaphoreType.DMA((steps,)),
                pltpu.SemaphoreType.DMA((steps,)),
                pltpu.SemaphoreType.DMA((steps,)),
                pltpu.SemaphoreType.DMA((steps,)),
                pltpu.SemaphoreType.DMA((3,)),
                pltpu.SemaphoreType.DMA((3,)),
                pltpu.SemaphoreType.DMA((2,)),
                pltpu.SemaphoreType.DMA((ITERS,)),
                pltpu.SemaphoreType.DMA((ITERS,)),
            ],
            compiler_params=pltpu.CompilerParams(
                collective_id=0, has_side_effects=True, vmem_limit_bytes=49 * 1024 * 1024),
        )(sharpness, fraction, density, cell_kind)
        threshold = level[0, :1]
        physical = 0.5 * (1.0 + jnp.tanh(sharpness[0] * (coded - threshold[0])))
        return physical, threshold

    in_specs = (P("slab", "pencil", None), P("slab", "pencil", None), P(), P())
    out_specs = (P("slab", "pencil", None), P())
    return jax.shard_map(local, mesh=mesh, in_specs=in_specs, out_specs=out_specs, check_vma=False)
```

profile of v0, /device:TPU:1, one launch (start us, length us, event | category | flops | bytes accessed | tf_op | source)
XLA Modules:
  0.0 201.3 jit_solution(16390415452156187530)
XLA Ops:
  1.9 195.8 %shard_map.59 = (f32[6,384,384]{2,1,0:T(8,128)S(1)}, f32[1,128]{1,0:T(1,128)S(1)}) custom-call(f32[1]{0:T(128)} %copy.7.beta_ref, f32[1]{0:T(128)S(6)} %copy.8.fraction_ref, f32[6,384,384]{2,1,0:T(8,128)} %density.1, s32[6,384,384]{2,1,0:T(8,128)} %kind.1), custom_call_target="tpu_custom_call" | custom-call | tf_op jit(solution)/shard_map/pallas_call | solution.py:319
  197.7 2.4 %add_multiply_fusion = f32[6,384,384]{2,1,0:T(8,128)} fusion(f32[6,384,384]{2,1,0:T(8,128)S(1)} %get-tuple-element.4, f32[]{:T(128)S(1)} %bitcast.5, f32[]{:T(128)} %bitcast.4), kind=kLoop, calls=%fused_computation | loop fusion | flops 3538944 | bytes 7077896 | tf_op jit(solution)/shard_map/mul | solution.py:349
where the time goes:
time: 201 us
  Pallas kernels  196 us (98%)
  between operations  3.09 us (2%)
  other arithmetic  2.4 us (1%)
    pallas_call x1, Pallas kernels, local(): pl.pallas_call(functools.partial(kernel, slabs, pencils), out_shape=(jax....  196 us

commit v1 on v0

--- a/solution.py
+++ b/solution.py
@@ -11,8 +11,7 @@
 ITERS = 3
 CHUNK = 16
 PAD = 8
-WINDOW = 4
-LEAD = 8
+WINDOW = 6
 LANES = 128
 FAR = 1.0e6
 MESH = pl.DeviceIdType.MESH
@@ -53,16 +52,12 @@
     return tiles[0]
 
 
-def kernel(slabs, pencils, beta_ref, fraction_ref, density, kind, coded, level_out, own, near, far, kinds,
-           along_z, x_band, acc, parts, x_send, x_recv, b_send, b_recv, f_send, f_recv, h_send, h_recv, local_sem,
-           r_send, r_recv):
+def kernel(slabs, pencils, beta_ref, fraction_ref, density, kind, coded, level_out, own, below, above, kinds,
+           along_z, x_band, acc, parts, u_send, u_recv, d_send, d_recv, h_send, h_recv, local_sem, r_send, r_recv):
     depth, rows, cols = density.shape
     steps = rows // CHUNK
-    lead = min(LEAD, steps)
-    lag = lead + 1
     slab = lax.axis_index("slab")
     pencil = lax.axis_index("pencil")
-    even = slab % 2 == 0
     first = pencil == 0
     devices = slabs * pencils
     me = slab * pencils + pencil
@@ -79,12 +74,10 @@
     lax.fori_loop(1, slabs, greet, 0, unroll=15 if slabs % 15 == 1 else 1)
     pl.semaphore_signal(barrier, inc=1, device_id=(slab, 1 - pencil), device_id_type=MESH)
 
-    partner = slab + jnp.where(even, 1, -1)
-    target = slab + jnp.where(even, 2, -2)
-    source = slab - jnp.where(even, 2, -2)
-    has_target = (target >= 0) & (target < slabs)
-    has_source = (source >= 0) & (source < slabs)
-    target = jnp.clip(target, 0, slabs - 1)
+    has_above = slab + 1 < slabs
+    has_below = slab > 0
+    upper = jnp.minimum(slab + 1, slabs - 1)
+    lower = jnp.maximum(slab - 1, 0)
     sibling = 1 - pencil
     halo = pl.multiple_of(jnp.where(first, PAD + rows, 0), 8)
     edge = pl.multiple_of(jnp.where(first, 0, PAD + rows), 8)
@@ -94,26 +87,17 @@
     def row_of(k):
         return pl.multiple_of(jnp.where(first, steps - 1 - k, k) * CHUNK, CHUNK)
 
-    def x_copy(k):
+    def up_copy(k):
         r = row_of(k)
-        layers = pl.ds(jnp.where(even, 0, depth - RADIUS), RADIUS)
         return pltpu.make_async_remote_copy(
-            density.at[layers, pl.ds(r, CHUNK), :], near.at[layers, pl.ds(r + PAD, CHUNK), :],
-            x_send.at[k], x_recv.at[k], device_id=(partner, pencil), device_id_type=MESH)
-
-    def b_copy(k):
+            density.at[pl.ds(depth - RADIUS, RADIUS), pl.ds(r, CHUNK), :], below.at[:, pl.ds(r + PAD, CHUNK), :],
+            u_send.at[k], u_recv.at[k], device_id=(upper, pencil), device_id_type=MESH)
+
+    def down_copy(k):
         r = row_of(k)
-        layers = pl.ds(jnp.where(even, RADIUS, 0), depth - RADIUS)
         return pltpu.make_async_remote_copy(
-            density.at[layers, pl.ds(r, CHUNK), :], near.at[layers, pl.ds(r + PAD, CHUNK), :],
-            b_send.at[k], b_recv.at[k], device_id=(partner, pencil), device_id_type=MESH)
-
-    def f_copy(k):
-        r = row_of(k)
-        start = jnp.where(even, depth - RADIUS, 0)
-        return pltpu.make_async_remote_copy(
-            near.at[pl.ds(start, RADIUS), pl.ds(r + PAD, CHUNK), :], far.at[:, pl.ds(r + PAD, CHUNK), :],
-            f_send.at[k], f_recv.at[k], device_id=(target, pencil), device_id_type=MESH)
+            density.at[pl.ds(0, RADIUS), pl.ds(r, CHUNK), :], above.at[:, pl.ds(r + PAD, CHUNK), :],
+            d_send.at[k], d_recv.at[k], device_id=(lower, pencil), device_id_type=MESH)
 
     def halo_copy(index, src, dst):
         return pltpu.make_async_remote_copy(
@@ -121,27 +105,43 @@
 
     own_row = pl.multiple_of(jnp.where(first, rows - PAD, 0), 8)
     own_halo = halo_copy(0, density.at[:, pl.ds(own_row, PAD), :], own.at[:, pl.ds(there, PAD), :])
-    near_halo = halo_copy(1, near.at[:, pl.ds(mine, PAD), :], near.at[:, pl.ds(there, PAD), :])
-    far_halo = halo_copy(2, far.at[:, pl.ds(mine, PAD), :], far.at[:, pl.ds(there, PAD), :])
+    below_halo = halo_copy(1, below.at[:, pl.ds(mine, PAD), :], below.at[:, pl.ds(there, PAD), :])
+    above_halo = halo_copy(2, above.at[:, pl.ds(mine, PAD), :], above.at[:, pl.ds(there, PAD), :])
     own_load = pltpu.make_async_copy(density, own.at[:, pl.ds(PAD, rows), :], local_sem.at[0])
     kind_load = pltpu.make_async_copy(kind, kinds, local_sem.at[1])
 
     own_load.start()
     kind_load.start()
     pl.semaphore_wait(barrier, devices - 1)
+
+    def send_chunk(k):
+        @pl.when(has_above)
+        def _():
+            up_copy(k).start()
+
+        @pl.when(has_below)
+        def _():
+            down_copy(k).start()
+
     for k in range(min(WINDOW, steps)):
-        x_copy(k).start()
+        send_chunk(k)
     own_halo.start()
 
     x_band[...] = band((cols, cols), 0)
     acc[...] = jnp.zeros_like(acc)
     along_z[:, pl.ds(edge, PAD), :] = jnp.zeros((depth, PAD, cols), jnp.float32)
 
-    @pl.when(jnp.logical_not(has_source))
+    @pl.when(jnp.logical_not(has_below))
     def _():
         @pl.loop(0, RADIUS)
         def _(k):
-            far[k] = jnp.zeros(far.shape[1:], jnp.float32)
+            below[k] = jnp.zeros(below.shape[1:], jnp.float32)
+
+    @pl.when(jnp.logical_not(has_above))
+    def _():
+        @pl.loop(0, RADIUS)
+        def _(k):
+            above[k] = jnp.zeros(above.shape[1:], jnp.float32)
 
     beta = beta_ref[0]
 
@@ -149,11 +149,11 @@
         for r in range(0, count, 8):
             for c in range(0, cols, LANES):
                 at = (pl.ds(pl.multiple_of(start + r, 8), 8), pl.ds(c, LANES))
-                values = [far[jnp.where(even, m, RADIUS - 1 - m), at[0], at[1]] for m in range(RADIUS)]
-                values += [own[jnp.where(even, i, depth - 1 - i), at[0], at[1]] for i in range(depth)]
-                values += [near[jnp.where(even, i, depth - 1 - i), at[0], at[1]] for i in range(RADIUS)]
+                values = [below[m, at[0], at[1]] for m in range(RADIUS)]
+                values += [own[i, at[0], at[1]] for i in range(depth)]
+                values += [above[i, at[0], at[1]] for i in range(RADIUS)]
                 for i, out in enumerate(box(box(values))):
-                    along_z[jnp.where(even, i, depth - 1 - i), at[0], at[1]] = out
+                    along_z[i, at[0], at[1]] = out
 
     def filter_yx(j):
         r = row_of(j)
@@ -181,67 +181,54 @@
             acc[0] += folded(tangent)
             acc[1] += folded(1.0 - tangent * tangent)
 
-    @pl.loop(0, steps + lag + 1)
+    @pl.loop(0, steps + 1)
     def _(k):
         @pl.when(k < steps)
         def _():
-            x_copy(k).wait_recv()
-
-            @pl.when(has_target)
-            def _():
-                f_copy(k).start()
-
-        @pl.when(k + WINDOW < steps)
-        def _():
-            x_copy(k + WINDOW).start()
-
-            @pl.when(k + WINDOW >= lead)
-            def _():
-                b_copy(k + WINDOW - lead).start()
-
-        @pl.when(k + WINDOW == steps)
-        def _():
-            @pl.loop(max(steps - lead, 0), steps)
-            def _(j):
-                b_copy(j).start()
-
-        @pl.when((k >= lag) & (k < steps + lag))
-        def _():
-            b_copy(k - lag).wait_recv()
-
-            @pl.when(k == lag)
-            def _():
-                near_halo.start()
-
-            @pl.when(has_source)
-            def _():
-                f_copy(k - lag).wait_recv()
-
-                @pl.when(k == lag)
+            @pl.when(k + WINDOW < steps)
+            def _():
+                send_chunk(k + WINDOW)
+
+            @pl.when(has_below)
+            def _():
+                up_copy(k).wait_recv()
+
+                @pl.when(k == 0)
                 def _():
-                    far_halo.start()
-
-            @pl.when(k == lag)
+                    below_halo.start()
+
+            @pl.when(has_above)
+            def _():
+                down_copy(k).wait_recv()
+
+                @pl.when(k == 0)
+                def _():
+                    above_halo.start()
+
+            @pl.when(k == 0)
             def _():
                 own_load.wait()
                 kind_load.wait()
 
-            filter_z(row_of(k - lag) + PAD, CHUNK)
-
-        @pl.when(k == lag + 1)
+            filter_z(row_of(k) + PAD, CHUNK)
+
+        @pl.when(k == 1)
         def _():
             own_halo.wait_recv()
-            near_halo.wait_recv()
-
-            @pl.when(has_source)
-            def _():
-                far_halo.wait_recv()
+
+            @pl.when(has_below)
+            def _():
+                below_halo.wait_recv()
+
+            @pl.when(has_above)
+            def _():
+                above_halo.wait_recv()
 
             filter_z(halo, PAD)
 
-        @pl.when(k >= lag + 1)
-        def _():
-            filter_yx(k - lag - 1)
+        @pl.when(k >= 1)
+        def _():
+            filter_yx(k - 1)
 
     cells = float(devices) * float(depth * rows * cols)
     level = jnp.full((1, 1), 0.5, jnp.float32)
@@ -290,19 +277,23 @@
 
     @pl.loop(0, steps)
     def _(k):
-        x_copy(k).wait_send()
-        b_copy(k).wait_send()
-
-        @pl.when(has_target)
-        def _():
-            f_copy(k).wait_send()
+        @pl.when(has_above)
+        def _():
+            up_copy(k).wait_send()
+
+        @pl.when(has_below)
+        def _():
+            down_copy(k).wait_send()
 
     own_halo.wait_send()
-    near_halo.wait_send()
-
-    @pl.when(has_source)
+
+    @pl.when(has_below)
     def _():
-        far_halo.wait_send()
+        below_halo.wait_send()
+
+    @pl.when(has_above)
+    def _():
+        above_halo.wait_send()
 
     for step in range(ITERS):
         most = parts.at[step, pl.ds(0, devices - 1)]
@@ -323,15 +314,13 @@
             out_specs=(pl.BlockSpec(memory_space=pltpu.VMEM), pl.BlockSpec(memory_space=pltpu.VMEM)),
             scratch_shapes=[
                 pltpu.VMEM((depth, wide, cols), jnp.float32),
-                pltpu.VMEM((depth, wide, cols), jnp.float32),
+                pltpu.VMEM((RADIUS, wide, cols), jnp.float32),
                 pltpu.VMEM((RADIUS, wide, cols), jnp.float32),
                 pltpu.VMEM((depth, rows, cols), jnp.int32),
                 pltpu.VMEM((depth, wide, cols), jnp.float32),
                 pltpu.VMEM((cols, cols), jnp.bfloat16),
                 pltpu.VMEM((2, 8, LANES), jnp.float32),
                 pltpu.VMEM((ITERS, slabs * pencils, 2, LANES), jnp.float32),
-                pltpu.SemaphoreType.DMA((steps,)),
-                pltpu.SemaphoreType.DMA((steps,)),
                 pltpu.SemaphoreType.DMA((steps,)),
                 pltpu.SemaphoreType.DMA((steps,)),
                 pltpu.SemaphoreType.DMA((steps,)),

time: 201 us -> 125 us (0.62)
  Pallas kernels: 196 us -> 119 us
    pallas_call x1, Pallas kernels: 196 us -> 119 us  [local(): pl.pallas_call(functools.partial(kernel, slabs, pencils), out_shape=(jax....]
where the time goes in v1:
time: 125 us
  Pallas kernels  119 us (95%)
  between operations  3.09 us (2%)
  other arithmetic  2.4 us (2%)
    pallas_call x1, Pallas kernels, local(): pl.pallas_call(functools.partial(kernel, slabs, pencils), out_shape=(jax....  119 us

profile of v1, /device:TPU:1, one launch (start us, length us, event | category | flops | bytes accessed | tf_op | source)
XLA Modules:
  0.0 124.8 jit_solution(6790124132837226638)
XLA Ops:
  1.9 119.3 %shard_map.59 = (f32[6,384,384]{2,1,0:T(8,128)S(1)}, f32[1,128]{1,0:T(1,128)S(1)}) custom-call(f32[1]{0:T(128)} %copy.7.beta_ref, f32[1]{0:T(128)S(6)} %copy.8.fraction_ref, f32[6,384,384]{2,1,0:T(8,128)} %density.1, s32[6,384,384]{2,1,0:T(8,128)} %kind.1), custom_call_target="tpu_custom_call" | custom-call | tf_op jit(solution)/shard_map/pallas_call | solution.py:310
  121.3 2.4 %add_multiply_fusion = f32[6,384,384]{2,1,0:T(8,128)} fusion(f32[6,384,384]{2,1,0:T(8,128)S(1)} %get-tuple-element.4, f32[]{:T(128)S(1)} %bitcast.5, f32[]{:T(128)} %bitcast.4), kind=kLoop, calls=%fused_computation | loop fusion | flops 3538944 | bytes 7077896 | tf_op jit(solution)/shard_map/mul | solution.py:338

commit v2 on v1

--- a/solution.py
+++ b/solution.py
@@ -1,4 +1,6 @@
 import functools
+import itertools
+import math
 
 import jax
 import jax.numpy as jnp
@@ -11,8 +13,10 @@
 ITERS = 3
 CHUNK = 16
 PAD = 8
-WINDOW = 6
 LANES = 128
+HALF = 64
+WAIT = 5
+GRID = (4, 8, 4)
 FAR = 1.0e6
 MESH = pl.DeviceIdType.MESH
 
@@ -52,27 +56,34 @@
     return tiles[0]
 
 
-def kernel(slabs, pencils, beta_ref, fraction_ref, density, kind, coded, level_out, own, below, above, kinds,
-           along_z, x_band, acc, parts, u_send, u_recv, d_send, d_recv, h_send, h_recv, local_sem, r_send, r_recv):
+def distance(offset, sizes):
+    return sum(min(o, n - o) for o, n in zip(offset, sizes))
+
+
+def kernel(slabs, pencils, grid, beta_in, fraction_in, density, kind, coded, level_out, own, below, above, kinds,
+           along_z, x_band, acc, pair, parts, beta_ref, fraction_ref, u_send, u_recv, d_send, d_recv, h_send, h_recv,
+           local_sem, p_send, p_recv, r_send, r_recv, known):
     depth, rows, cols = density.shape
     steps = rows // CHUNK
+    reach = max((slabs - 1).bit_length() - 1, 1)
     slab = lax.axis_index("slab")
     pencil = lax.axis_index("pencil")
     first = pencil == 0
     devices = slabs * pencils
-    me = slab * pencils + pencil
 
     barrier = pltpu.get_barrier_semaphore()
 
-    def greet(k, carry):
-        there = slab + (slabs - k)
-        there = there - jnp.where(there >= slabs, slabs, 0)
-        for core in range(pencils):
-            pl.semaphore_signal(barrier, inc=1, device_id=(there, core), device_id_type=MESH)
-        return carry
-
-    lax.fori_loop(1, slabs, greet, 0, unroll=15 if slabs % 15 == 1 else 1)
+    def around(step):
+        there = slab + (step if step > 0 else slabs + step)
+        return there - jnp.where(there >= slabs, slabs, 0)
+
+    for step in (1, -1):
+        pl.semaphore_signal(barrier, inc=1, device_id=(around(step), pencil), device_id_type=MESH)
     pl.semaphore_signal(barrier, inc=1, device_id=(slab, 1 - pencil), device_id_type=MESH)
+
+    def spread(j):
+        for step in (1 << j, -(1 << j)):
+            pl.semaphore_signal(known.at[j], inc=1, device_id=(around(step), pencil), device_id_type=MESH)
 
     has_above = slab + 1 < slabs
     has_below = slab > 0
@@ -109,10 +120,14 @@
     above_halo = halo_copy(2, above.at[:, pl.ds(mine, PAD), :], above.at[:, pl.ds(there, PAD), :])
     own_load = pltpu.make_async_copy(density, own.at[:, pl.ds(PAD, rows), :], local_sem.at[0])
     kind_load = pltpu.make_async_copy(kind, kinds, local_sem.at[1])
+    beta_load = pltpu.make_async_copy(beta_in, beta_ref, local_sem.at[2])
+    fraction_load = pltpu.make_async_copy(fraction_in, fraction_ref, local_sem.at[3])
 
     own_load.start()
     kind_load.start()
-    pl.semaphore_wait(barrier, devices - 1)
+    beta_load.start()
+    fraction_load.start()
+    pl.semaphore_wait(barrier, 3)
 
     def send_chunk(k):
         @pl.when(has_above)
@@ -123,9 +138,10 @@
         def _():
             down_copy(k).start()
 
-    for k in range(min(WINDOW, steps)):
-        send_chunk(k)
+    send_chunk(0)
     own_halo.start()
+    pl.loop(1, steps)(send_chunk)
+    spread(0)
 
     x_band[...] = band((cols, cols), 0)
     acc[...] = jnp.zeros_like(acc)
@@ -143,6 +159,8 @@
         def _(k):
             above[k] = jnp.zeros(above.shape[1:], jnp.float32)
 
+    beta_load.wait()
+    fraction_load.wait()
     beta = beta_ref[0]
 
     def filter_z(start, count):
@@ -175,9 +193,9 @@
             cover = coverage(depth_index, slabs * depth) * cover_y * cover_x
             filtered = smoothed[layer * CHUNK : (layer + 1) * CHUNK] / cover
             which = kinds[layer, pl.ds(r, CHUNK), :]
-            value = jnp.where(which == 0, filtered, jnp.where(which == 2, FAR, -FAR))
+            value = jnp.where(which == 0, beta * filtered, jnp.where(which == 2, FAR, -FAR))
             coded[layer, pl.ds(r, CHUNK), :] = value
-            tangent = jnp.tanh(beta * (value - 0.5))
+            tangent = jnp.tanh(value - 0.5 * beta)
             acc[0] += folded(tangent)
             acc[1] += folded(1.0 - tangent * tangent)
 
@@ -185,10 +203,6 @@
     def _(k):
         @pl.when(k < steps)
         def _():
-            @pl.when(k + WINDOW < steps)
-            def _():
-                send_chunk(k + WINDOW)
-
             @pl.when(has_below)
             def _():
                 up_copy(k).wait_recv()
@@ -230,16 +244,39 @@
         def _():
             filter_yx(k - 1)
 
+        for j in range(reach):
+            @pl.when(k == WAIT + j)
+            def _():
+                pl.semaphore_wait(known.at[j], 2)
+                if j + 1 < reach:
+                    spread(j + 1)
+
     cells = float(devices) * float(depth * rows * cols)
+    offsets = [o for o in itertools.product(*(range(n) for n in grid)) if any(o)]
+    offsets.sort(key=lambda o: -distance(o, grid))
+    far_half = offsets[: slabs // 2]
+    near_half = offsets[slabs // 2 :]
+    lane = lax.broadcasted_iota(jnp.int32, (1, LANES), 1)
+
+    def shifted(offset):
+        there, place, scale = 0, slab, slabs
+        for o, n in zip(offset, grid):
+            scale //= n
+            at = place // scale
+            place = place - at * scale
+            at = at + o
+            there = there + jnp.where(at >= n, at - n, at) * scale
+        return there
+
     level = jnp.full((1, 1), 0.5, jnp.float32)
     for step in range(ITERS):
         if step:
-            center = jnp.broadcast_to(level, (8, cols))
+            center = jnp.broadcast_to(beta * level, (8, cols))
 
             def body(i, carry):
                 total, bend = carry
                 for layer in range(depth):
-                    tangent = jnp.tanh(beta * (coded[layer, pl.ds(pl.multiple_of(i * 8, 8), 8), :] - center))
+                    tangent = jnp.tanh(coded[layer, pl.ds(pl.multiple_of(i * 8, 8), 8), :] - center)
                     total = total + tangent
                     bend = bend + (1.0 - tangent * tangent)
                 return total, bend
@@ -249,29 +286,36 @@
             total, bend = folded(total), folded(bend)
         else:
             total, bend = acc[0], acc[1]
-        parts[step, me] = jnp.concatenate(
-            [jnp.sum(total, axis=0, keepdims=True), jnp.sum(bend, axis=0, keepdims=True)], axis=0)
+        total = jnp.sum(total, axis=0, keepdims=True)
+        bend = jnp.sum(bend, axis=0, keepdims=True)
+        total = total + pltpu.roll(total, HALF, 1)
+        bend = bend + pltpu.roll(bend, HALF, 1)
+        pair[step, 0] = jnp.where(lane < HALF, total, bend)
+        swap = pltpu.make_async_remote_copy(
+            pair.at[step, 0], pair.at[step, 1], p_send.at[step], p_recv.at[step],
+            device_id=(slab, sibling), device_id_type=MESH)
+        swap.start()
+        swap.wait_recv()
+        parts[step, slab] = pair[step, 0] + pair[step, 1]
 
         def send(there, core):
             pltpu.make_async_remote_copy(
-                parts.at[step, me], parts.at[step, me], r_send.at[step], r_recv.at[step],
+                parts.at[step, slab], parts.at[step, slab], r_send.at[step], r_recv.at[step],
                 device_id=(there, core), device_id_type=MESH).start()
 
-        def send_all(k, carry):
-            there = slab + (slabs - k)
-            there = there - jnp.where(there >= slabs, slabs, 0)
-            for core in range(pencils):
-                send(there, core)
-            return carry
-
-        lax.fori_loop(1, slabs, send_all, 0, unroll=15 if slabs % 15 == 1 else 1)
-        send(slab, sibling)
-
-        most = parts.at[step, pl.ds(0, devices - 1)]
+        for here, chips in ((pencils - 1, far_half), (0, near_half)):
+            @pl.when(pencil == here)
+            def _():
+                for offset in chips:
+                    there = shifted(offset)
+                    for core in range(pencils):
+                        send(there, core)
+
+        most = parts.at[step, pl.ds(0, slabs - 1)]
         pltpu.make_async_copy(most, most, r_recv.at[step]).wait()
-        both = jnp.sum(jnp.sum(parts[step], axis=0), axis=1, keepdims=True)
-        volume = 0.5 * (cells + both[0:1])
-        slope = cells + 0.5 * beta * both[1:2]
+        both = jnp.sum(parts[step], axis=0)
+        volume = 0.5 * (cells + jnp.sum(jnp.where(lane < HALF, both, 0.0), axis=1, keepdims=True))
+        slope = cells + 0.5 * beta * jnp.sum(jnp.where(lane < HALF, 0.0, both), axis=1, keepdims=True)
         level = level + (volume - fraction_ref[0] * cells) / slope
     level_out[...] = jnp.broadcast_to(level, level_out.shape)
 
@@ -296,21 +340,29 @@
         above_halo.wait_send()
 
     for step in range(ITERS):
-        most = parts.at[step, pl.ds(0, devices - 1)]
-        pltpu.make_async_copy(most, most, r_send.at[step]).wait()
+        pltpu.make_async_copy(pair.at[step, 0], pair.at[step, 0], p_send.at[step]).wait()
+
+    for here, chips in ((pencils - 1, far_half), (0, near_half)):
+        @pl.when(pencil == here)
+        def _():
+            for step in range(ITERS):
+                most = parts.at[step, pl.ds(0, len(chips))]
+                for core in range(pencils):
+                    pltpu.make_async_copy(most, most, r_send.at[step]).wait()
 
 
 def solution(mesh):
     slabs, pencils = mesh.shape["slab"], mesh.shape["pencil"]
+    grid = GRID if math.prod(GRID) == slabs else (slabs,)
 
     def local(density, cell_kind, sharpness, fraction):
         depth, rows, cols = density.shape
         steps = rows // CHUNK
         wide = rows + 2 * PAD
         coded, level = pl.pallas_call(
-            functools.partial(kernel, slabs, pencils),
+            functools.partial(kernel, slabs, pencils, grid),
             out_shape=(jax.ShapeDtypeStruct(density.shape, jnp.float32), jax.ShapeDtypeStruct((1, LANES), jnp.float32)),
-            in_specs=[pl.BlockSpec(memory_space=pltpu.SMEM)] * 2 + [pl.BlockSpec(memory_space=pltpu.HBM)] * 2,
+            in_specs=[pl.BlockSpec(memory_space=pltpu.HBM)] * 4,
             out_specs=(pl.BlockSpec(memory_space=pltpu.VMEM), pl.BlockSpec(memory_space=pltpu.VMEM)),
             scratch_shapes=[
                 pltpu.VMEM((depth, wide, cols), jnp.float32),
@@ -320,22 +372,28 @@
                 pltpu.VMEM((depth, wide, cols), jnp.float32),
                 pltpu.VMEM((cols, cols), jnp.bfloat16),
                 pltpu.VMEM((2, 8, LANES), jnp.float32),
-                pltpu.VMEM((ITERS, slabs * pencils, 2, LANES), jnp.float32),
+                pltpu.VMEM((ITERS, 2, 1, LANES), jnp.float32),
+                pltpu.VMEM((ITERS, slabs, 1, LANES), jnp.float32),
+                pltpu.SMEM((1,), jnp.float32),
+                pltpu.SMEM((1,), jnp.float32),
                 pltpu.SemaphoreType.DMA((steps,)),
                 pltpu.SemaphoreType.DMA((steps,)),
                 pltpu.SemaphoreType.DMA((steps,)),
                 pltpu.SemaphoreType.DMA((steps,)),
                 pltpu.SemaphoreType.DMA((3,)),
                 pltpu.SemaphoreType.DMA((3,)),
-                pltpu.SemaphoreType.DMA((2,)),
+                pltpu.SemaphoreType.DMA((4,)),
                 pltpu.SemaphoreType.DMA((ITERS,)),
                 pltpu.SemaphoreType.DMA((ITERS,)),
+                pltpu.SemaphoreType.DMA((ITERS,)),
+                pltpu.SemaphoreType.DMA((ITERS,)),
+                pltpu.SemaphoreType.REGULAR((max((slabs - 1).bit_length() - 1, 1),)),
             ],
             compiler_params=pltpu.CompilerParams(
                 collective_id=0, has_side_effects=True, vmem_limit_bytes=49 * 1024 * 1024),
         )(sharpness, fraction, density, cell_kind)
         threshold = level[0, :1]
-        physical = 0.5 * (1.0 + jnp.tanh(sharpness[0] * (coded - threshold[0])))
+        physical = 0.5 * (1.0 + jnp.tanh(coded - sharpness[0] * threshold[0]))
         return physical, threshold
 
     in_specs = (P("slab", "pencil", None), P("slab", "pencil", None), P(), P())

time: 125 us -> 111 us (0.89)
  Pallas kernels: 119 us -> 106 us
    pallas_call x1, Pallas kernels: 119 us -> 106 us  [local(): pl.pallas_call(functools.partial(kernel, slabs, pencils, grid), out_shape...]
where the time goes in v2:
time: 111 us
  Pallas kernels  106 us (95%)
  between operations  3.13 us (3%)
  other arithmetic  2.26 us (2%)
    pallas_call x1, Pallas kernels, local(): pl.pallas_call(functools.partial(kernel, slabs, pencils, grid), out_shape...  106 us
    mul x1, other arithmetic, local(): physical = 0.5 * (1.0 + jnp.tanh(coded - sharpness[0] * threshold[0]))  2.26 us

profile of v2, /device:TPU:1, one launch (start us, length us, event | category | flops | bytes accessed | tf_op | source)
XLA Modules:
  0.0 111.0 jit_solution(17419527067506110461)
XLA Ops:
  1.9 105.6 %shard_map.59 = (f32[6,384,384]{2,1,0:T(8,128)S(1)}, f32[1,128]{1,0:T(1,128)S(1)}) custom-call(f32[1]{0:T(128)} %copy.7.beta_in, f32[1]{0:T(128)S(6)} %copy.8.fraction_in, f32[6,384,384]{2,1,0:T(8,128)} %density.1, s32[6,384,384]{2,1,0:T(8,128)} %kind.1), custom_call_target="tpu_custom_call" | custom-call | tf_op jit(solution)/shard_map/pallas_call | solution.py:362
  107.5 2.3 %add_multiply_fusion = f32[6,384,384]{2,1,0:T(8,128)} fusion(f32[6,384,384]{2,1,0:T(8,128)S(1)} %get-tuple-element.4, f32[]{:T(128)S(6)} %mul.9), kind=kLoop, calls=%fused_computation | loop fusion | flops 2654208 | bytes 7077892 | tf_op jit(solution)/shard_map/mul | solution.py:396

commit v3 on v2

--- a/solution.py
+++ b/solution.py
@@ -47,13 +47,15 @@
     return jnp.maximum(RADIUS + 1 - jnp.abs(col - shift - row), 0).astype(jnp.float32).astype(jnp.bfloat16)
 
 
+def tree(parts):
+    parts = list(parts)
+    while len(parts) > 1:
+        parts = [sum(parts[i : i + 2][1:], parts[i]) for i in range(0, len(parts), 2)]
+    return parts[0]
+
+
 def folded(x):
-    tiles = [
-        x[i : i + 8, j : j + LANES] for i in range(0, x.shape[0], 8) for j in range(0, x.shape[1], LANES)
-    ]
-    while len(tiles) > 1:
-        tiles = [sum(tiles[i : i + 2][1:], tiles[i]) for i in range(0, len(tiles), 2)]
-    return tiles[0]
+    return tree(x[i : i + 8, j : j + LANES] for i in range(0, x.shape[0], 8) for j in range(0, x.shape[1], LANES))
 
 
 def distance(offset, sizes):
@@ -254,8 +256,11 @@
     cells = float(devices) * float(depth * rows * cols)
     offsets = [o for o in itertools.product(*(range(n) for n in grid)) if any(o)]
     offsets.sort(key=lambda o: -distance(o, grid))
-    far_half = offsets[: slabs // 2]
-    near_half = offsets[slabs // 2 :]
+    direct = [o for o in offsets if distance(o, grid) >= sum(n // 2 for n in grid) - 1]
+    rest = offsets[len(direct) :]
+    far_half = rest[: (len(rest) + 1) // 2]
+    near_half = rest[(len(rest) + 1) // 2 :]
+    arrivals = slabs - 1 + len(direct)
     lane = lax.broadcasted_iota(jnp.int32, (1, LANES), 1)
 
     def shifted(offset):
@@ -265,29 +270,35 @@
             at = place // scale
             place = place - at * scale
             at = at + o
-            there = there + jnp.where(at >= n, at - n, at) * scale
+            there = there + jnp.where(at >= n, at - n, jnp.where(at < 0, at + n, at)) * scale
         return there
 
-    level = jnp.full((1, 1), 0.5, jnp.float32)
-    for step in range(ITERS):
-        if step:
-            center = jnp.broadcast_to(beta * level, (8, cols))
+    def send(step, source, slot, there, core):
+        pltpu.make_async_remote_copy(
+            source, parts.at[step, slot], r_send.at[step], r_recv.at[step],
+            device_id=(there, core), device_id_type=MESH).start()
+
+    def newton(step, level):
+        @pl.when(step > 0)
+        def _():
+            center = jnp.broadcast_to(beta * level, (8, LANES))
 
             def body(i, carry):
                 total, bend = carry
+                at = pl.ds(pl.multiple_of(i * 8, 8), 8)
                 for layer in range(depth):
-                    tangent = jnp.tanh(coded[layer, pl.ds(pl.multiple_of(i * 8, 8), 8), :] - center)
-                    total = total + tangent
-                    bend = bend + (1.0 - tangent * tangent)
+                    tangents = [jnp.tanh(coded[layer, at, pl.ds(c * LANES, LANES)] - center) for c in range(cols // LANES)]
+                    total = tuple(a + t for a, t in zip(total, tangents))
+                    bend = tuple(a + (1.0 - t * t) for a, t in zip(bend, tangents))
                 return total, bend
 
-            zero = jnp.zeros((8, cols), jnp.float32)
-            total, bend = lax.fori_loop(0, rows // 8, body, (zero, zero), unroll=2)
-            total, bend = folded(total), folded(bend)
-        else:
-            total, bend = acc[0], acc[1]
-        total = jnp.sum(total, axis=0, keepdims=True)
-        bend = jnp.sum(bend, axis=0, keepdims=True)
+            zero = (jnp.zeros((8, LANES), jnp.float32),) * (cols // LANES)
+            total, bend = lax.fori_loop(0, rows // 8, body, (zero, zero), unroll=6)
+            acc[0] = tree(total)
+            acc[1] = tree(bend)
+
+        total = jnp.sum(acc[0], axis=0, keepdims=True)
+        bend = jnp.sum(acc[1], axis=0, keepdims=True)
         total = total + pltpu.roll(total, HALF, 1)
         bend = bend + pltpu.roll(bend, HALF, 1)
         pair[step, 0] = jnp.where(lane < HALF, total, bend)
@@ -295,13 +306,12 @@
             pair.at[step, 0], pair.at[step, 1], p_send.at[step], p_recv.at[step],
             device_id=(slab, sibling), device_id_type=MESH)
         swap.start()
+        for j, offset in enumerate(direct):
+            there = shifted(offset)
+            for core in range(pencils):
+                send(step, pair.at[step, 0], jnp.where(first, slab, slabs + j), there, core)
         swap.wait_recv()
         parts[step, slab] = pair[step, 0] + pair[step, 1]
-
-        def send(there, core):
-            pltpu.make_async_remote_copy(
-                parts.at[step, slab], parts.at[step, slab], r_send.at[step], r_recv.at[step],
-                device_id=(there, core), device_id_type=MESH).start()
 
         for here, chips in ((pencils - 1, far_half), (0, near_half)):
             @pl.when(pencil == here)
@@ -309,15 +319,21 @@
                 for offset in chips:
                     there = shifted(offset)
                     for core in range(pencils):
-                        send(there, core)
-
-        most = parts.at[step, pl.ds(0, slabs - 1)]
+                        send(step, parts.at[step, slab], slab, there, core)
+
+        most = parts.at[step, pl.ds(0, arrivals)]
         pltpu.make_async_copy(most, most, r_recv.at[step]).wait()
-        both = jnp.sum(parts[step], axis=0)
+        for j, offset in enumerate(direct):
+            there = shifted([-o for o in offset])
+            parts[step, there] = parts[step, there] + parts[step, slabs + j]
+        both = tree([parts[step, i] for i in range(slabs)])
         volume = 0.5 * (cells + jnp.sum(jnp.where(lane < HALF, both, 0.0), axis=1, keepdims=True))
         slope = cells + 0.5 * beta * jnp.sum(jnp.where(lane < HALF, 0.0, both), axis=1, keepdims=True)
-        level = level + (volume - fraction_ref[0] * cells) / slope
-    level_out[...] = jnp.broadcast_to(level, level_out.shape)
+        return level + (volume - fraction_ref[0] * cells) / slope
+
+    level = lax.fori_loop(0, ITERS, newton, jnp.full((1, LANES), 0.5, jnp.float32))
+    level_out[0:1] = level
+    level_out[1:2] = beta * level
 
     @pl.loop(0, steps)
     def _(k):
@@ -346,9 +362,30 @@
         @pl.when(pencil == here)
         def _():
             for step in range(ITERS):
-                most = parts.at[step, pl.ds(0, len(chips))]
+                most = parts.at[step, pl.ds(0, len(direct) + len(chips))]
                 for core in range(pencils):
                     pltpu.make_async_copy(most, most, r_send.at[step]).wait()
+
+
+def project(coded, level, physical, threshold, held, level_held, sems, level_sem):
+    depth, rows, cols = coded.shape
+    center = jnp.broadcast_to(level[1:2], (8, LANES))
+    level_held[0] = jnp.max(level[0:1])
+    level_copy = pltpu.make_async_copy(level_held, threshold, level_sem)
+    level_copy.start()
+    copies = []
+    for layer in range(depth):
+        @pl.loop(0, rows // 8, unroll=16)
+        def _(i):
+            at = pl.ds(pl.multiple_of(i * 8, 8), 8)
+            for c in range(0, cols, LANES):
+                held[layer, at, pl.ds(c, LANES)] = 0.5 * (1.0 + jnp.tanh(coded[layer, at, pl.ds(c, LANES)] - center))
+
+        copies.append(pltpu.make_async_copy(held.at[layer], physical.at[layer], sems.at[layer]))
+        copies[-1].start()
+    for copy in copies:
+        copy.wait()
+    level_copy.wait()
 
 
 def solution(mesh):
@@ -361,7 +398,7 @@
         wide = rows + 2 * PAD
         coded, level = pl.pallas_call(
             functools.partial(kernel, slabs, pencils, grid),
-            out_shape=(jax.ShapeDtypeStruct(density.shape, jnp.float32), jax.ShapeDtypeStruct((1, LANES), jnp.float32)),
+            out_shape=(jax.ShapeDtypeStruct(density.shape, jnp.float32), jax.ShapeDtypeStruct((2, LANES), jnp.float32)),
             in_specs=[pl.BlockSpec(memory_space=pltpu.HBM)] * 4,
             out_specs=(pl.BlockSpec(memory_space=pltpu.VMEM), pl.BlockSpec(memory_space=pltpu.VMEM)),
             scratch_shapes=[
@@ -373,7 +410,7 @@
                 pltpu.VMEM((cols, cols), jnp.bfloat16),
                 pltpu.VMEM((2, 8, LANES), jnp.float32),
                 pltpu.VMEM((ITERS, 2, 1, LANES), jnp.float32),
-                pltpu.VMEM((ITERS, slabs, 1, LANES), jnp.float32),
+                pltpu.VMEM((ITERS, 2 * slabs, 1, LANES), jnp.float32),
                 pltpu.SMEM((1,), jnp.float32),
                 pltpu.SMEM((1,), jnp.float32),
                 pltpu.SemaphoreType.DMA((steps,)),
@@ -392,9 +429,19 @@
             compiler_params=pltpu.CompilerParams(
                 collective_id=0, has_side_effects=True, vmem_limit_bytes=49 * 1024 * 1024),
         )(sharpness, fraction, density, cell_kind)
-        threshold = level[0, :1]
-        physical = 0.5 * (1.0 + jnp.tanh(coded - sharpness[0] * threshold[0]))
-        return physical, threshold
+        return pl.pallas_call(
+            project,
+            out_shape=(jax.ShapeDtypeStruct(density.shape, jnp.float32), jax.ShapeDtypeStruct((1,), jnp.float32)),
+            in_specs=[pl.BlockSpec(memory_space=pltpu.VMEM)] * 2,
+            out_specs=(pl.BlockSpec(memory_space=pltpu.HBM), pl.BlockSpec(memory_space=pltpu.HBM)),
+            scratch_shapes=[
+                pltpu.VMEM(density.shape, jnp.float32),
+                pltpu.SMEM((1,), jnp.float32),
+                pltpu.SemaphoreType.DMA((depth,)),
+                pltpu.SemaphoreType.DMA,
+            ],
+            compiler_params=pltpu.CompilerParams(vmem_limit_bytes=8 * 1024 * 1024),
+        )(coded, level)
 
     in_specs = (P("slab", "pencil", None), P("slab", "pencil", None), P(), P())
     out_specs = (P("slab", "pencil", None), P())

time: 111 us -> 108 us (0.973)
  other arithmetic: 2.26 us -> 0 us
  between operations: 3.13 us -> 1.93 us
    mul x1 -> x0, other arithmetic: 2.26 us -> none  [local(): physical = 0.5 * (1.0 + jnp.tanh(coded - sharpness[0] * threshold[0]))]
    pallas_call x0 -> x1, Pallas kernels: none -> 2.11 us  [local(): pl.pallas_call(project, out_shape=(jax.ShapeDtypeStruct(density.shape, jn...]
    pallas_call x1, Pallas kernels: 106 us -> 104 us  [local(): pl.pallas_call(functools.partial(kernel, slabs, pencils, grid), out_shape...]
where the time goes in v3:
time: 108 us
  Pallas kernels  106 us (98%)
  between operations  1.93 us (2%)
    pallas_call x1, Pallas kernels, local(): pl.pallas_call(functools.partial(kernel, slabs, pencils, grid), out_shape...  104 us

profile of v3, /device:TPU:1, one launch (start us, length us, event | category | flops | bytes accessed | tf_op | source)
XLA Modules:
  0.0 108.3 jit_solution(13911652460631767983)
XLA Ops:
  1.9 104.2 %shard_map.59 = (f32[6,384,384]{2,1,0:T(8,128)S(1)}, f32[2,128]{1,0:T(2,128)S(1)}) custom-call(f32[1]{0:T(128)S(6)} %copy.6.beta_in, f32[1]{0:T(128)S(6)} %copy.7.fraction_in, f32[6,384,384]{2,1,0:T(8,128)} %density.1, s32[6,384,384]{2,1,0:T(8,128)} %kind.1), custom_call_target="tpu_custom_call" | custom-call | tf_op jit(solution)/shard_map/pallas_call | solution.py:399
  106.1 2.1 %shard_map.60 = (f32[6,384,384]{2,1,0:T(8,128)}, f32[1]{0:T(128)}) custom-call(f32[6,384,384]{2,1,0:T(8,128)S(1)} %get-tuple-element.4.coded, f32[2,128]{1,0:T(2,128)S(1)} %get-tuple-element.5.level), custom_call_target="tpu_custom_call" | custom-call | tf_op jit(solution)/shard_map/pallas_call | solution.py:432

commit v4 on v3

--- a/solution.py
+++ b/solution.py
@@ -15,6 +15,7 @@
 PAD = 8
 LANES = 128
 HALF = 64
+NEARER = 2
 WAIT = 5
 GRID = (4, 8, 4)
 FAR = 1.0e6
@@ -140,10 +141,9 @@
         def _():
             down_copy(k).start()
 
-    send_chunk(0)
+    pl.loop(0, steps)(send_chunk)
+    parts[:, slabs:] = jnp.zeros((ITERS, slabs, 1, LANES), jnp.float32)
     own_halo.start()
-    pl.loop(1, steps)(send_chunk)
-    spread(0)
 
     x_band[...] = band((cols, cols), 0)
     acc[...] = jnp.zeros_like(acc)
@@ -246,6 +246,10 @@
         def _():
             filter_yx(k - 1)
 
+        @pl.when(k == WAIT - 1)
+        def _():
+            spread(0)
+
         for j in range(reach):
             @pl.when(k == WAIT + j)
             def _():
@@ -256,10 +260,10 @@
     cells = float(devices) * float(depth * rows * cols)
     offsets = [o for o in itertools.product(*(range(n) for n in grid)) if any(o)]
     offsets.sort(key=lambda o: -distance(o, grid))
-    direct = [o for o in offsets if distance(o, grid) >= sum(n // 2 for n in grid) - 1]
+    direct = [o for o in offsets if distance(o, grid) >= sum(n // 2 for n in grid) - NEARER]
     rest = offsets[len(direct) :]
-    far_half = rest[: (len(rest) + 1) // 2]
-    near_half = rest[(len(rest) + 1) // 2 :]
+    far_half = rest[0::2]
+    near_half = rest[1::2]
     arrivals = slabs - 1 + len(direct)
     lane = lax.broadcasted_iota(jnp.int32, (1, LANES), 1)
 
@@ -306,10 +310,10 @@
             pair.at[step, 0], pair.at[step, 1], p_send.at[step], p_recv.at[step],
             device_id=(slab, sibling), device_id_type=MESH)
         swap.start()
-        for j, offset in enumerate(direct):
+        for offset in direct:
             there = shifted(offset)
             for core in range(pencils):
-                send(step, pair.at[step, 0], jnp.where(first, slab, slabs + j), there, core)
+                send(step, pair.at[step, 0], pencil * slabs + slab, there, core)
         swap.wait_recv()
         parts[step, slab] = pair[step, 0] + pair[step, 1]
 
@@ -321,12 +325,31 @@
                     for core in range(pencils):
                         send(step, parts.at[step, slab], slab, there, core)
 
+        @pl.when(step == 0)
+        def _():
+            @pl.loop(0, steps)
+            def _(k):
+                @pl.when(has_above)
+                def _():
+                    up_copy(k).wait_send()
+
+                @pl.when(has_below)
+                def _():
+                    down_copy(k).wait_send()
+
+            own_halo.wait_send()
+
+            @pl.when(has_below)
+            def _():
+                below_halo.wait_send()
+
+            @pl.when(has_above)
+            def _():
+                above_halo.wait_send()
+
         most = parts.at[step, pl.ds(0, arrivals)]
         pltpu.make_async_copy(most, most, r_recv.at[step]).wait()
-        for j, offset in enumerate(direct):
-            there = shifted([-o for o in offset])
-            parts[step, there] = parts[step, there] + parts[step, slabs + j]
-        both = tree([parts[step, i] for i in range(slabs)])
+        both = tree([parts[step, i] + parts[step, slabs + i] for i in range(slabs)])
         volume = 0.5 * (cells + jnp.sum(jnp.where(lane < HALF, both, 0.0), axis=1, keepdims=True))
         slope = cells + 0.5 * beta * jnp.sum(jnp.where(lane < HALF, 0.0, both), axis=1, keepdims=True)
         return level + (volume - fraction_ref[0] * cells) / slope
@@ -334,26 +357,6 @@
     level = lax.fori_loop(0, ITERS, newton, jnp.full((1, LANES), 0.5, jnp.float32))
     level_out[0:1] = level
     level_out[1:2] = beta * level
-
-    @pl.loop(0, steps)
-    def _(k):
-        @pl.when(has_above)
-        def _():
-            up_copy(k).wait_send()
-
-        @pl.when(has_below)
-        def _():
-            down_copy(k).wait_send()
-
-    own_halo.wait_send()
-
-    @pl.when(has_below)
-    def _():
-        below_halo.wait_send()
-
-    @pl.when(has_above)
-    def _():
-        above_halo.wait_send()
 
     for step in range(ITERS):
         pltpu.make_async_copy(pair.at[step, 0], pair.at[step, 0], p_send.at[step]).wait()

time: 108 us -> 108 us (level)
  no operation moved by 1% of the time
where the time goes in v4:
time: 108 us
  Pallas kernels  106 us (98%)
  between operations  1.93 us (2%)
    pallas_call x1, Pallas kernels, local(): pl.pallas_call(functools.partial(kernel, slabs, pencils, grid), out_shape...  104 us

profile of v4, /device:TPU:1, one launch (start us, length us, event | category | flops | bytes accessed | tf_op | source)
XLA Modules:
  0.0 107.7 jit_solution(9588465202057663300)
XLA Ops:
  1.9 103.7 %shard_map.59 = (f32[6,384,384]{2,1,0:T(8,128)S(1)}, f32[2,128]{1,0:T(2,128)S(1)}) custom-call(f32[1]{0:T(128)S(6)} %copy.6.beta_in, f32[1]{0:T(128)S(6)} %copy.7.fraction_in, f32[6,384,384]{2,1,0:T(8,128)} %density.1, s32[6,384,384]{2,1,0:T(8,128)} %kind.1), custom_call_target="tpu_custom_call" | custom-call | tf_op jit(solution)/shard_map/pallas_call | solution.py:402
  105.6 2.1 %shard_map.60 = (f32[6,384,384]{2,1,0:T(8,128)}, f32[1]{0:T(128)}) custom-call(f32[6,384,384]{2,1,0:T(8,128)S(1)} %get-tuple-element.4.coded, f32[2,128]{1,0:T(2,128)S(1)} %get-tuple-element.5.level), custom_call_target="tpu_custom_call" | custom-call | tf_op jit(solution)/shard_map/pallas_call | solution.py:435

commit v5 on v4

--- a/solution.py
+++ b/solution.py
@@ -377,14 +377,18 @@
     level_copy = pltpu.make_async_copy(level_held, threshold, level_sem)
     level_copy.start()
     copies = []
-    for layer in range(depth):
-        @pl.loop(0, rows // 8, unroll=16)
+    half = rows // 2
+    for piece in range(2 * depth):
+        layer, start = piece // 2, piece % 2 * half
+
+        @pl.loop(0, half // 8, unroll=12)
         def _(i):
-            at = pl.ds(pl.multiple_of(i * 8, 8), 8)
+            at = pl.ds(pl.multiple_of(start + i * 8, 8), 8)
             for c in range(0, cols, LANES):
                 held[layer, at, pl.ds(c, LANES)] = 0.5 * (1.0 + jnp.tanh(coded[layer, at, pl.ds(c, LANES)] - center))
 
-        copies.append(pltpu.make_async_copy(held.at[layer], physical.at[layer], sems.at[layer]))
+        band_rows = pl.ds(start, half)
+        copies.append(pltpu.make_async_copy(held.at[layer, band_rows], physical.at[layer, band_rows], sems.at[piece]))
         copies[-1].start()
     for copy in copies:
         copy.wait()
@@ -440,7 +444,7 @@
             scratch_shapes=[
                 pltpu.VMEM(density.shape, jnp.float32),
                 pltpu.SMEM((1,), jnp.float32),
-                pltpu.SemaphoreType.DMA((depth,)),
+                pltpu.SemaphoreType.DMA((2 * depth,)),
                 pltpu.SemaphoreType.DMA,
             ],
             compiler_params=pltpu.CompilerParams(vmem_limit_bytes=8 * 1024 * 1024),

time: 108 us -> 108 us (level)
  no operation moved by 1% of the time
where the time goes in v5:
time: 108 us
  Pallas kernels  106 us (98%)
  between operations  1.93 us (2%)
    pallas_call x1, Pallas kernels, local(): pl.pallas_call(functools.partial(kernel, slabs, pencils, grid), out_shape...  104 us

profile of v5, /device:TPU:1, one launch (start us, length us, event | category | flops | bytes accessed | tf_op | source)
XLA Modules:
  0.0 107.7 jit_solution(13104848745436477462)
XLA Ops:
  1.9 103.7 %shard_map.59 = (f32[6,384,384]{2,1,0:T(8,128)S(1)}, f32[2,128]{1,0:T(2,128)S(1)}) custom-call(f32[1]{0:T(128)S(6)} %copy.6.beta_in, f32[1]{0:T(128)S(6)} %copy.7.fraction_in, f32[6,384,384]{2,1,0:T(8,128)} %density.1, s32[6,384,384]{2,1,0:T(8,128)} %kind.1), custom_call_target="tpu_custom_call" | custom-call | tf_op jit(solution)/shard_map/pallas_call | solution.py:406
  105.6 2.1 %shard_map.60 = (f32[6,384,384]{2,1,0:T(8,128)}, f32[1]{0:T(128)}) custom-call(f32[6,384,384]{2,1,0:T(8,128)S(1)} %get-tuple-element.4.coded, f32[2,128]{1,0:T(2,128)S(1)} %get-tuple-element.5.level), custom_call_target="tpu_custom_call" | custom-call | tf_op jit(solution)/shard_map/pallas_call | solution.py:439
